TPU v7x, 32 devices: a whole 2x2x4 slice. The times are simulated.
32 devices in a mesh: cuts: 4 (over y, x), space: 8 (over z, core).
Axes of the slice: x: 2, y: 2, z: 4, core: 2. Of those that a mesh axis runs over, the one named last changes fastest.
Arguments:
- starts: float32 [4, 3, 32, 64, 128], P('cuts', None, 'space'), may hold values from -3 to 3
Outputs:
- new_starts: float32 [4, 3, 32, 64, 128], P('cuts', None, 'space')
All inputs are finite; a program needn't handle non-finite values.
Results may differ from a plain program's by a relative error of at most 0.0001.
Values sent between devices are 32-bit elements; how exact they have to be, the bound alone decides.
A program may use at most 64 MiB of HBM per device.

v0:
```python
import functools

import jax
import jax.numpy as jnp
from jax import lax
from jax.experimental import pallas as pl
from jax.experimental.pallas import tpu as pltpu
from jax.sharding import PartitionSpec as P

FSTEPS = 16
CSTEPS = 2

fine_rate = 0.08
fine_advect = 0.04
coarse_rate = 0.16
coarse_advect = 0.16

PAD = 8
MESH = pl.DeviceIdType.MESH


def step(src, dst, items, rows, rate, advect, shift, turn):
    lanes = src.shape[-1]
    lane = lax.broadcasted_iota(jnp.int32, (8, lanes), 1)
    first, last = lane < shift, lane >= lanes - shift
    rzp, azp = jnp.where(last, 0.0, rate), jnp.where(last, 0.0, advect)
    rzm, azm = jnp.where(first, 0.0, rate), jnp.where(first, 0.0, advect)
    for row in range(rows[0], rows[1], 8):
        for si, di, keep in items:
            v = [src[si, c, pl.ds(row, 8), :] for c in range(3)]
            ax, ay = (advect * turn) * v[0], advect * v[1]
            xp, xm, yp, ym = rate - ax, rate + ax, rate - ay, rate + ay
            zp, zm = rzp - azp * v[2], rzm + azm * v[2]
            for c in range(3):
                x_part = xp * src[si + 1, c, pl.ds(row, 8), :] + xm * src[si - 1, c, pl.ds(row, 8), :]
                y_part = yp * src[si, c, pl.ds(row + 1, 8), :] + ym * src[si, c, pl.ds(row - 1, 8), :]
                z_part = zp * pltpu.roll(v[c], lanes - shift, 1) + zm * pltpu.roll(v[c], shift, 1)
                value = ((1.0 - 6.0 * rate) * v[c] + x_part) + (y_part + z_part)
                dst[di, c, pl.ds(row, 8), :] = value if keep is None else value * keep


def kernel(S, N, x_ref, out_ref, ev, od, ca, cb, cc, pk_old, pk_r, pk_cs, pk_adv, rc_old, rc_own, rc_z, rc_r, rc_rz, rc_r1,
           rc_adv, rc_end, spread, load_sem, halo_s, halo_r, part_s, part_r, mid_s, mid_r, end_s, end_r, old_s, old_r,
           own_s, own_r, z_s, z_r, r_s, r_r, rz_s, rz_r, r1_s, r1_r,
           adv_s, adv_r):
    n, s = lax.axis_index("cuts"), lax.axis_index("space")
    W, NY, NZ = x_ref.shape[2], x_ref.shape[3], x_ref.shape[4]
    CW, CY, Q, D = W // 2, NY // 2, 4 * W, 2 * W
    ROUNDS = FSTEPS // D
    END = FSTEPS // 2
    p = lax.rem(s, 2)
    way = 1 - 2 * p
    turn = way.astype(jnp.float32)
    near, mate = s - way, s + way
    far, beyond = s - 2 * way, s + 2 * way
    wall = (near < 0) | (near >= S)
    mate_wall = (beyond < 0) | (beyond >= S)
    inside = jnp.logical_not(wall)
    mate_inside = jnp.logical_not(mate_wall)
    works = n < N - 1

    def wrap(i):
        return lax.rem(i + 2 * S, S)

    def column(i):
        return lax.rem(i, N)

    pairs = [(n, near, inside), (n, mate, n >= 0)]
    pairs += [(n, far, inside & (n >= 3)), (n, beyond, mate_inside & (n >= 3))]
    pairs += [(n + 1, s, n < N - 1), (n - 1, s, n > 0)]
    pairs += [(n + 2, s, (n > 0) & (n < N - 2)), (n - 2, s, n > 2)]
    pairs += [(n + 3, s, n == 0), (n - 3, s, n == 3)]
    barrier = pltpu.get_barrier_semaphore()
    count = 0
    for i, j, cond in pairs:
        @pl.when(cond)
        def _():
            pl.semaphore_signal(barrier, inc=1, device_id=(i, j), device_id_type=MESH)
        count = count + jnp.where(cond, 1, 0)

    inner = pl.ds(PAD, NY)

    def load(i):
        return pltpu.make_async_copy(x_ref.at[0, :, i + p * (W - 1 - 2 * i)], ev.at[D + i, :, inner], load_sem.at[i])

    keep_start = pltpu.make_async_copy(x_ref.at[0], out_ref.at[0], load_sem.at[W])

    @pl.when(works)
    def _():
        for i in range(W):
            load(i).start()

    @pl.when(n == 0)
    def _():
        keep_start.start()

    zero = jnp.zeros((PAD, NZ), jnp.float32)

    def clear(i, _):
        for c in range(3):
            for top in (0, PAD + NY):
                ev[i, c, pl.ds(top, PAD), :] = zero
                od[i, c, pl.ds(top, PAD), :] = zero
        return 0

    def clear_layer(i, _):
        for c in range(3):
            for row in range(PAD, PAD + NY, 8):
                ev[i * Q + D - 1, c, pl.ds(row, 8), :] = zero
                od[i * Q + D - 1, c, pl.ds(row, 8), :] = zero
        return 0

    def clear_start(i, _):
        for c in range(3):
            for row in range(PAD, PAD + NY, 8):
                ev[i, c, pl.ds(row, 8), :] = zero
        return 0

    def clear_coarse(i, _):
        for c in range(3):
            for top in (0, PAD + CY):
                ca[i, c, pl.ds(top, PAD), :] = zero
                cb[i, c, pl.ds(top, PAD), :] = zero
        return 0

    lax.fori_loop(0, END * Q, clear, 0)
    lax.fori_loop(0, jnp.where(wall, END, 0), clear_layer, 0)
    lax.fori_loop(0, jnp.where(wall, D, 0), clear_start, 0)
    lax.fori_loop(0, 5 * CW, clear_coarse, 0)

    @pl.when(works)
    def _():
        for i in range(W):
            load(i).wait()

    pl.semaphore_wait(barrier, count)

    def remote(src, dst, send_sem, recv_sem, target):
        return pltpu.make_async_remote_copy(
            src_ref=src, dst_ref=dst, send_sem=send_sem, recv_sem=recv_sem, device_id=target, device_id_type=MESH)

    def halo(r, d):
        at = r * W * Q
        return remote(ev.at[at + D + d, :, inner], ev.at[at + D - 1 - d, :, inner], halo_s.at[r, d], halo_r.at[r, d],
                      (n, wrap(near)))

    def to_mate(r, i):
        at = r * W * Q
        return remote(ev.at[at + D + i, :, inner], ev.at[at + Q - 1 - i, :, inner], part_s.at[r, i], part_r.at[r, i],
                      (n, wrap(mate)))

    def mid_to_mate(r, i):
        at = (r * W + CW) * Q
        return remote(ev.at[at + D + i, :, inner], ev.at[at + Q - 1 - i, :, inner], mid_s.at[r, i], mid_r.at[r, i],
                      (n, wrap(mate)))

    def send_halo(r, d):
        @pl.when(inside)
        def _():
            halo(r, d).start()

    def to_next(i):
        return remote(ev.at[END * Q + D + i, :, inner], rc_end.at[i], end_s.at[i], end_r.at[i], (column(n + 1), s))

    even = lax.broadcasted_iota(jnp.int32, (CY, NZ), 1) % 2 == 0
    crow = pl.ds(PAD, CY)

    def restricted(at, c):
        def read(l, r):
            return ev[at + l, c, pl.ds(PAD + r, CY, stride=2), :]
        total = (read(0, 0) + read(0, 1)) + (read(1, 0) + read(1, 1))
        other = jnp.where(even, pltpu.roll(total, NZ - 1, 1), pltpu.roll(total, 1, 1))
        return (total + other) * 0.125

    def packed(a, b):
        return jnp.where(even, a, b)

    def unpacked(v):
        return jnp.where(even, v, pltpu.roll(v, 1, 1)), jnp.where(even, pltpu.roll(v, NZ - 1, 1), v)

    near_keep = jnp.where(wall, jnp.zeros((8, NZ), jnp.float32), 1.0)
    beyond_keep = jnp.where(mate_wall, jnp.zeros((8, NZ), jnp.float32), 1.0)

    def coarse(src, dst, lo, hi):
        items = [(c, c, near_keep if c < 2 * CW else beyond_keep if c >= 4 * CW else None) for c in range(lo, hi)]
        step(src, dst, items, (PAD, PAD + CY), coarse_rate, coarse_advect, 2, turn)

    def fine(at, l, qs):
        e, o = ev.at[pl.ds(at, W * Q + 2 * D)], od.at[pl.ds(at, (W - 1) * Q + 2 * D)]
        src, dst = (e, o) if l % 2 else (o, e)
        step(src, dst, [((l - 1) // 2 * Q + q, l // 2 * Q + q, None) for q in qs], (PAD, PAD + NY), fine_rate, fine_advect, 1, turn)

    send_old = remote(pk_old, rc_old, old_s, old_r, (column(n + 1), s))

    def one_round(r, _):
        base = r * W
        for m in range(W):
            i = W - 1 - m
            if m == 0:
                @pl.when(r == 0)
                def _():
                    to_mate(r, i).wait_recv()
                    send_halo(r, W)
            else:
                to_mate(r, i).wait_recv()
                send_halo(r, W + m)
        for l in range(1, W):
            def pair(h, _):
                fine(base * Q + 2 * h, l, [D + l, D + l + 1])
                return 0
            lax.fori_loop(0, W - l, pair, 0)

        @pl.when(r == ROUNDS - 1)
        def _():
            def restrict_layer(c, _):
                for k in range(3):
                    ca[c, k, crow, :] = restricted(2 * c, k)
                return 0
            lax.fori_loop(CW, 4 * CW, restrict_layer, 0)
            coarse(ca, cb, 2 * CW - 1, 3 * CW + 1)
            coarse(cb, cc, 2 * CW, 3 * CW)
            for k in range(3):
                pk_old[k] = packed(cc[2 * CW, k, crow, :], cc[2 * CW + 1, k, crow, :])
            send_old.start()

        def wave(k, levels):
            at = base * Q + D - 1 - k

            @pl.when(inside)
            def _():
                for l in levels:
                    fine(at, l, [l])

            @pl.when(wall)
            def _():
                for l in levels:
                    @pl.when(l > k)
                    def _():
                        fine(at, l, [l])

        def await_halo(k):
            @pl.when(inside)
            def _():
                halo(r, k).wait_recv()

        def early(k, _):
            await_halo(k)
            wave(k, range(1, W + 1))

            @pl.when(k < W)
            def _():
                mid_to_mate(r, W - 1 - k).start()

            @pl.when(k >= 1)
            def _():
                mid_to_mate(r, W - k).wait_recv()

            @pl.when(k >= 2)
            def _():
                for l in range(W + 1, D):
                    fine(base * Q + k, l, [Q - 1 - l])

            @pl.when(k >= 1)
            def _():
                wave(k, range(W + 1, D))
            return 0

        lax.fori_loop(0, W + 1, early, 0)
        wave(W, [D])

        def sent(k):
            i = D - 1 - k

            @pl.when(r < ROUNDS - 1)
            def _():
                to_mate(r + 1, i).start()
                if k == W:
                    send_halo(r + 1, i)
                elif k == W + 1:
                    send_halo(r + 1, i)
                    to_mate(r + 1, W - 1).wait_recv()
                    send_halo(r + 1, W)
                elif k == D - 1:
                    send_halo(r + 1, 0)
                    send_halo(r + 1, 1)

            @pl.when(r == ROUNDS - 1)
            def _():
                if k == W:
                    to_next(i).start()

        sent(W)

        def late(k, _):
            await_halo(k)
            wave(k, range(1, D + 1))
            for j in range(W + 1, D):
                @pl.when(k == j)
                def _():
                    sent(j)
            return 0

        lax.fori_loop(W + 1, D, late, 0)
        return 0

    def own_copy(target):
        return remote(pk_cs, rc_own, own_s, own_r, (column(target), s))

    adv_copy = remote(pk_adv, rc_adv, adv_s, adv_r, (column(n + N - 1), s))

    def r_copy(target):
        return remote(pk_r, rc_r, r_s, r_r, (column(target), s))

    def r1_copy(target):
        return remote(pk_r, rc_r1, r1_s, r1_r, (column(target), s))

    @pl.when(works)
    def _():
        for i in range(W):
            send_halo(0, i)
            to_mate(0, W - 1 - i).start()
        lax.fori_loop(0, ROUNDS, one_round, 0)
        for k in range(3):
            change = [restricted(END * Q + D + 2 * j, k) - cc[2 * CW + j, k, crow, :] for j in range(CW)]
            pk_r[k] = packed(*change)
            pk_cs[k] = packed(*(cc[2 * CW + j, k, crow, :] + change[j] for j in range(CW)))

        @pl.when(n == 0)
        def _():
            own_copy(3).start()

        @pl.when((n >= 1) & (n <= N - 3))
        def _():
            r_copy(n + 2).start()
        if N > 4:
            @pl.when((n >= 1) & (n <= N - 4))
            def _():
                r1_copy(n + 1).start()
        for i in range(W - 2, -1, -1):
            to_next(i).start()

    def exchange(src, dst, send, recv, k):
        target, slot = [(near, 0), (mate, 1), (far, 3), (beyond, 2)][k]
        return remote(src, dst.at[slot], send.at[slot], recv.at[slot], (n, wrap(target)))

    exists = [inside, None, inside, mate_inside]

    def guarded(cond, do):
        if cond is None:
            do()
        else:
            pl.when(cond)(do)

    places = [(2 * CW - 1, -1), (4 * CW - 1, -1), (0, 1), (4 * CW, 1)]
    slot_exists = [inside, None, inside, mate_inside]

    def unpack_into(dst, slot, src):
        first, by = places[slot]

        def fill():
            for k in range(3):
                for j, v in enumerate(unpacked(src[k])):
                    dst[first + by * j, k, crow, :] = v

        def blank():
            for k in range(3):
                for j in range(CW):
                    dst[first + by * j, k, crow, :] = jnp.zeros((CY, NZ), jnp.float32)

        guarded(slot_exists[slot], fill)
        if slot_exists[slot] is not None:
            pl.when(jnp.logical_not(slot_exists[slot]))(blank)

    @pl.when(n == 1)
    def _():
        old_copy = remote(pk_old, rc_old, old_s, old_r, (column(n + 1), s))
        old_copy.wait_recv()
        for k in range(3):
            for j, v in enumerate(unpacked(rc_old[k])):
                cc[2 * CW + j, k, crow, :] = v

    @pl.when(n == 2)
    def _():
        adv_copy.wait_recv()
        for k in range(3):
            for j, v in enumerate(unpacked(rc_adv[k])):
                cc[2 * CW + j, k, crow, :] = v

    @pl.when(n >= 3)
    def _():
        own_copy(n + 2).wait_recv()
        for k in range(4):
            guarded(exists[k], lambda: exchange(rc_own, rc_z, z_s, z_r, k).start())
        for k in range(3):
            for j, v in enumerate(unpacked(rc_own[k])):
                ca[2 * CW + j, k, crow, :] = v
        r_copy(n + 2).wait_recv()
        for k in range(2):
            guarded(exists[k], lambda: exchange(rc_r, rc_rz, rz_s, rz_r, k).start())
        for k, slot in ((1, 1), (0, 0), (2, 3), (3, 2)):
            guarded(slot_exists[slot], lambda: exchange(rc_own, rc_z, z_s, z_r, k).wait_recv())
            unpack_into(ca, slot, rc_z.at[slot])
        coarse(ca, cb, 1, 5 * CW - 1)
        coarse(cb, cc, CW, 4 * CW)

        @pl.when(n == 3)
        def _():
            for k in range(3):
                pk_adv[k] = packed(cc[2 * CW, k, crow, :], cc[2 * CW + 1, k, crow, :])
            adv_copy.start()
        for slot in (1, 0):
            guarded(slot_exists[slot], lambda: exchange(rc_r, rc_rz, rz_s, rz_r, slot).wait_recv())
            unpack_into(ca, slot, rc_rz.at[slot])
        for k in range(3):
            for j, v in enumerate(unpacked(rc_r[k])):
                ca[2 * CW + j, k, crow, :] = v

        def add(c, _):
            for k in range(3):
                ca[c, k, crow, :] = ca[c, k, crow, :] + cc[c, k, crow, :]
            return 0

        lax.fori_loop(CW, 4 * CW, add, 0)
        coarse(ca, cb, 2 * CW - 1, 3 * CW + 1)
        coarse(cb, cc, 2 * CW, 3 * CW)

    if N > 4:
        @pl.when((n >= 2) & (n <= N - 3))
        def _():
            r1_copy(n + 1).wait_recv()
            for k in range(3):
                change = unpacked(rc_r1[k])
                pk_cs[k] = packed(*(cc[2 * CW + j, k, crow, :] + change[j] for j in range(CW)))
            own_copy(n + 2).start()

    @pl.when(n == 0)
    def _():
        keep_start.wait()

    @pl.when(n > 0)
    def _():
        @pl.when(n > 1)
        def _():
            send_old.wait_recv()
        for k in range(3):
            old = unpacked(rc_old[k])
            for j in range(CW):
                rise = cc[2 * CW + j, k, crow, :] - old[j]
                for r in range(2):
                    spread[j, k, pl.ds(r, CY, stride=2), :] = rise
        for i in range(W - 1, -1, -1):
            to_next(i).wait_recv()
            for k in range(3):
                out_ref[0, k, i + p * (W - 1 - 2 * i)] = spread[i // 2, k, pl.ds(0, NY), :] + rc_end[i, k]

    @pl.when(works)
    def _():
        send_old.wait_send()
        for i in range(W):
            to_next(i).wait_send()
            for r in range(ROUNDS):
                to_mate(r, i).wait_send()
                mid_to_mate(r, i).wait_send()

        @pl.when(inside)
        def _():
            for r in range(ROUNDS):
                for d in range(D):
                    halo(r, d).wait_send()

        @pl.when(n == 0)
        def _():
            own_copy(3).wait_send()

        @pl.when((n >= 1) & (n <= N - 3))
        def _():
            r_copy(n + 2).wait_send()
        if N > 4:
            @pl.when((n >= 1) & (n <= N - 4))
            def _():
                r1_copy(n + 1).wait_send()

            @pl.when((n >= 2) & (n <= N - 3))
            def _():
                own_copy(n + 2).wait_send()

    @pl.when(n >= 3)
    def _():
        for k in range(4):
            guarded(exists[k], lambda: exchange(rc_own, rc_z, z_s, z_r, k).wait_send())
        for k in range(2):
            guarded(exists[k], lambda: exchange(rc_r, rc_rz, rz_s, rz_r, k).wait_send())

        @pl.when(n == 3)
        def _():
            adv_copy.wait_send()


def shards(S, N, starts):
    W, NY, NZ = starts.shape[2:]
    D, Q = 2 * W, 4 * W
    assert W == 4 and FSTEPS % D == 0 and CSTEPS == 2 and S % 2 == 0 and N > 3
    f32 = jnp.float32
    CW, CY, ROUNDS, END = W // 2, NY // 2, FSTEPS // D, FSTEPS // 2
    pack = (3, CY, NZ)
    coarse = pltpu.VMEM((5 * CW, 3, CY + 2 * PAD, NZ), f32)
    dma = pltpu.SemaphoreType.DMA
    return pl.pallas_call(
        functools.partial(kernel, S, N),
        out_shape=jax.ShapeDtypeStruct(starts.shape, f32),
        in_specs=[pl.BlockSpec(memory_space=pltpu.HBM)],
        out_specs=pl.BlockSpec(memory_space=pltpu.VMEM),
        scratch_shapes=[
            pltpu.VMEM(((END + 1) * Q + D, 3, NY + 2 * PAD, NZ), f32),
            pltpu.VMEM((END * Q + D, 3, NY + 2 * PAD, NZ), f32),
            coarse, coarse, coarse,
            pltpu.VMEM(pack, f32), pltpu.VMEM(pack, f32), pltpu.VMEM(pack, f32), pltpu.VMEM(pack, f32),
            pltpu.VMEM(pack, f32), pltpu.VMEM(pack, f32), pltpu.VMEM((4,) + pack, f32),
            pltpu.VMEM(pack, f32), pltpu.VMEM((2,) + pack, f32), pltpu.VMEM(pack, f32), pltpu.VMEM(pack, f32),
            pltpu.VMEM((W, 3, NY, NZ), f32),
            pltpu.VMEM((CW, 3, NY + PAD, NZ), f32),
            dma((W + 1,)),
            dma((ROUNDS, D)), dma((ROUNDS, D)), dma((ROUNDS, W)), dma((ROUNDS, W)), dma((ROUNDS, W)), dma((ROUNDS, W)),
            dma((W,)), dma((W,)), dma, dma, dma, dma, dma((4,)), dma((4,)), dma, dma, dma((2,)), dma((2,)), dma, dma, dma, dma,
        ],
        compiler_params=pltpu.CompilerParams(collective_id=0, has_side_effects=True, vmem_limit_bytes=48 * 2**20),
    )(starts)


def solution(mesh):
    placed = P("cuts", None, "space", None, None)
    return jax.shard_map(
        functools.partial(shards, mesh.shape["space"], mesh.shape["cuts"]),
        mesh=mesh, in_specs=(placed,), out_specs=placed, check_vma=False)
```

profile of v0, /device:TPU:4, one launch (start us, length us, event | category | flops | bytes accessed | tf_op | source)
XLA Modules:
  0.0 39.6 jit_solution(10634096038673007814)
XLA Ops:
  0.0 0.0 copy-start
  0.0 1.0 %copy-done = f32[1,3,4,64,128]{4,3,2,1,0:T(8,128)S(1)} copy-done((f32[1,3,4,64,128]{4,3,2,1,0:T(8,128)S(1)}, f32[1,3,4,64,128]{4,3,2,1,0:T(8,128)}, u32[]{:S(2)}) %copy-start) | copy-done | bytes 393240
  1.0 37.9 %shard_map.17 = f32[1,3,4,64,128]{4,3,2,1,0:T(8,128)S(1)} custom-call(f32[1,3,4,64,128]{4,3,2,1,0:T(8,128)S(1)} %copy-done), custom_call_target="tpu_custom_call" | custom-call | tf_op jit(solution)/shard_map/pallas_call | solution.py:508
  38.9 0.7 %copy.3 = f32[1,3,4,64,128]{4,3,2,1,0:T(8,128)} copy(f32[1,3,4,64,128]{4,3,2,1,0:T(8,128)S(1)} %shard_map.17) | data formatting | bytes 786432
Async XLA Ops:
  0.0 1.0 %copy-start = (f32[1,3,4,64,128]{4,3,2,1,0:T(8,128)S(1)}, f32[1,3,4,64,128]{4,3,2,1,0:T(8,128)}, u32[]{:S(2)}) copy-start(f32[1,3,4,64,128]{4,3,2,1,0:T(8,128)} %x_ref.1) | copy-start | bytes 1179652
where the time goes:
time: 39.8 us; the launch traced here: 39.6 us
  Pallas kernels  37.9 us (95%)
  local copies, waits for them, and re-layouts  1.74 us (4%)
    pallas_call x1, Pallas kernels, shards(): pl.pallas_call(functools.partial(kernel, S, N), out_shape=jax.ShapeDtypeS...  37.9 us
    unnamed x3, local copies, waits for them, and re-layouts  1.74 us

commit v1 on v0

--- a/solution.py
+++ b/solution.py
@@ -224,49 +224,39 @@
             send_old.start()
 
         def wave(k, levels):
-            at = base * Q + D - 1 - k
+            fixed = isinstance(k, int)
+            at, first = (base * Q, D - 1 - k) if fixed else (base * Q + D - 1 - k, 0)
 
             @pl.when(inside)
             def _():
                 for l in levels:
-                    fine(at, l, [l])
+                    fine(at, l, [first + l])
 
             @pl.when(wall)
             def _():
                 for l in levels:
-                    @pl.when(l > k)
-                    def _():
-                        fine(at, l, [l])
+                    if not fixed:
+                        @pl.when(l > k)
+                        def _():
+                            fine(at, l, [first + l])
+                    elif l > k:
+                        fine(at, l, [first + l])
 
         def await_halo(k):
             @pl.when(inside)
             def _():
                 halo(r, k).wait_recv()
 
-        def early(k, _):
+        for k in range(W + 1):
             await_halo(k)
             wave(k, range(1, W + 1))
-
-            @pl.when(k < W)
-            def _():
+            if k < W:
                 mid_to_mate(r, W - 1 - k).start()
-
-            @pl.when(k >= 1)
-            def _():
+            if k >= 1:
                 mid_to_mate(r, W - k).wait_recv()
-
-            @pl.when(k >= 2)
-            def _():
-                for l in range(W + 1, D):
-                    fine(base * Q + k, l, [Q - 1 - l])
-
-            @pl.when(k >= 1)
-            def _():
-                wave(k, range(W + 1, D))
-            return 0
-
-        lax.fori_loop(0, W + 1, early, 0)
-        wave(W, [D])
+                for l in range(W + 1, W + k):
+                    fine(base * Q, l, [Q - 1 + k - l])
+                wave(k, range(W + 1, W + 1 + k))
 
         def sent(k):
             i = D - 1 - k
@@ -288,6 +278,8 @@
             def _():
                 if k == W:
                     to_next(i).start()
+                elif i > 0:
+                    pl.when(n > 0)(lambda: to_next(i).start())
 
         sent(W)
 
@@ -336,8 +328,9 @@
             @pl.when((n >= 1) & (n <= N - 4))
             def _():
                 r1_copy(n + 1).start()
-        for i in range(W - 2, -1, -1):
-            to_next(i).start()
+        for i in range(W - 2, 0, -1):
+            pl.when(n == 0)(lambda: to_next(i).start())
+        to_next(0).start()
 
     def exchange(src, dst, send, recv, k):
         target, slot = [(near, 0), (mate, 1), (far, 3), (beyond, 2)][k]
@@ -397,17 +390,26 @@
         r_copy(n + 2).wait_recv()
         for k in range(2):
             guarded(exists[k], lambda: exchange(rc_r, rc_rz, rz_s, rz_r, k).start())
-        for k, slot in ((1, 1), (0, 0), (2, 3), (3, 2)):
+        def arrived(k, slot):
             guarded(slot_exists[slot], lambda: exchange(rc_own, rc_z, z_s, z_r, k).wait_recv())
             unpack_into(ca, slot, rc_z.at[slot])
-        coarse(ca, cb, 1, 5 * CW - 1)
-        coarse(cb, cc, CW, 4 * CW)
+
+        arrived(1, 1)
+        arrived(0, 0)
+        coarse(ca, cb, 2 * CW - 1, 3 * CW + 1)
+        coarse(cb, cc, 2 * CW, 3 * CW)
 
         @pl.when(n == 3)
         def _():
             for k in range(3):
                 pk_adv[k] = packed(cc[2 * CW, k, crow, :], cc[2 * CW + 1, k, crow, :])
             adv_copy.start()
+        arrived(2, 3)
+        arrived(3, 2)
+        for lo, hi in ((1, 2 * CW - 1), (3 * CW + 1, 5 * CW - 1)):
+            coarse(ca, cb, lo, hi)
+        for lo, hi in ((CW, 2 * CW), (3 * CW, 4 * CW)):
+            coarse(cb, cc, lo, hi)
         for slot in (1, 0):
             guarded(slot_exists[slot], lambda: exchange(rc_r, rc_rz, rz_s, rz_r, slot).wait_recv())
             unpack_into(ca, slot, rc_rz.at[slot])

time: 39.8 us -> 38 us (0.955)
  the two profiles are of different devices: /device:TPU:4 before, /device:TPU:5 now
where the time goes in v1:
time: 38 us; the launch traced here: 37.9 us
  Pallas kernels  36.1 us (95%)
  local copies, waits for them, and re-layouts  1.74 us (5%)
    pallas_call x1, Pallas kernels, shards(): pl.pallas_call(functools.partial(kernel, S, N), out_shape=jax.ShapeDtypeS...  36.1 us
    unnamed x3, local copies, waits for them, and re-layouts  1.74 us

profile of v1, /device:TPU:5, one launch (start us, length us, event | category | flops | bytes accessed | tf_op | source)
XLA Modules:
  0.0 37.9 jit_solution(6858122080449711307)
XLA Ops:
  0.0 0.0 copy-start
  0.0 1.0 %copy-done = f32[1,3,4,64,128]{4,3,2,1,0:T(8,128)S(1)} copy-done((f32[1,3,4,64,128]{4,3,2,1,0:T(8,128)S(1)}, f32[1,3,4,64,128]{4,3,2,1,0:T(8,128)}, u32[]{:S(2)}) %copy-start) | copy-done | bytes 393240
  1.0 36.1 %shard_map.17 = f32[1,3,4,64,128]{4,3,2,1,0:T(8,128)S(1)} custom-call(f32[1,3,4,64,128]{4,3,2,1,0:T(8,128)S(1)} %copy-done), custom_call_target="tpu_custom_call" | custom-call | tf_op jit(solution)/shard_map/pallas_call | solution.py:510
  37.1 0.7 %copy.3 = f32[1,3,4,64,128]{4,3,2,1,0:T(8,128)} copy(f32[1,3,4,64,128]{4,3,2,1,0:T(8,128)S(1)} %shard_map.17) | data formatting | bytes 786432
Async XLA Ops:
  0.0 1.0 %copy-start = (f32[1,3,4,64,128]{4,3,2,1,0:T(8,128)S(1)}, f32[1,3,4,64,128]{4,3,2,1,0:T(8,128)}, u32[]{:S(2)}) copy-start(f32[1,3,4,64,128]{4,3,2,1,0:T(8,128)} %x_ref.1) | copy-start | bytes 1179652

commit v2 on v1

--- a/solution.py
+++ b/solution.py
@@ -381,15 +381,18 @@
 
     @pl.when(n >= 3)
     def _():
+        r_copy(n + 2).wait_recv()
+        for k in range(2):
+            guarded(exists[k], lambda: exchange(rc_r, rc_rz, rz_s, rz_r, k).start())
         own_copy(n + 2).wait_recv()
-        for k in range(4):
+        for k in range(2):
             guarded(exists[k], lambda: exchange(rc_own, rc_z, z_s, z_r, k).start())
         for k in range(3):
             for j, v in enumerate(unpacked(rc_own[k])):
                 ca[2 * CW + j, k, crow, :] = v
-        r_copy(n + 2).wait_recv()
-        for k in range(2):
-            guarded(exists[k], lambda: exchange(rc_r, rc_rz, rz_s, rz_r, k).start())
+        for k in range(2, 4):
+            guarded(exists[k], lambda: exchange(rc_own, rc_z, z_s, z_r, k).start())
+
         def arrived(k, slot):
             guarded(slot_exists[slot], lambda: exchange(rc_own, rc_z, z_s, z_r, k).wait_recv())
             unpack_into(ca, slot, rc_z.at[slot])
@@ -526,7 +529,7 @@
             dma((W,)), dma((W,)), dma, dma, dma, dma, dma((4,)), dma((4,)), dma, dma, dma((2,)), dma((2,)), dma, dma, dma, dma,
         ],
         compiler_params=pltpu.CompilerParams(collective_id=0, has_side_effects=True, vmem_limit_bytes=48 * 2**20),
-    )(starts)
+    )(pltpu.with_memory_space_constraint(starts, pltpu.HBM))
 
 
 def solution(mesh):

time: 38 us -> 37 us (0.974)
  local copies, waits for them, and re-layouts: 1.74 us -> 0.75 us
    unnamed x3 -> x1, local copies, waits for them, and re-layouts: 1.74 us -> 0.75 us
where the time goes in v2:
time: 37 us; the launch traced here: 36.9 us
  Pallas kernels  36.1 us (98%)
  local copies, waits for them, and re-layouts  0.75 us (2%)
    pallas_call x1, Pallas kernels, shards(): pl.pallas_call(functools.partial(kernel, S, N), out_shape=jax.ShapeDtypeS...  36.1 us
    unnamed x1, local copies, waits for them, and re-layouts  0.75 us

profile of v2, /device:TPU:5, one launch (start us, length us, event | category | flops | bytes accessed | tf_op | source)
XLA Modules:
  0.0 36.9 jit_solution(13816490479542968980)
XLA Ops:
  0.0 36.1 %shard_map.17 = f32[1,3,4,64,128]{4,3,2,1,0:T(8,128)S(1)} custom-call(f32[1,3,4,64,128]{4,3,2,1,0:T(8,128)} %x_ref.1), custom_call_target="tpu_custom_call" | custom-call | tf_op jit(solution)/shard_map/pallas_call | solution.py:513
  36.1 0.7 %copy.3 = f32[1,3,4,64,128]{4,3,2,1,0:T(8,128)} copy(f32[1,3,4,64,128]{4,3,2,1,0:T(8,128)S(1)} %shard_map.17) | data formatting | bytes 786432
